TPU v7x, 32 devices: a whole 2x2x4 slice. The times are simulated.
32 devices in a mesh: group: 2 (over y), temp: 4 (over x, core), gz: 4 (over z).
Axes of the slice: x: 2, y: 2, z: 4, core: 2. Of those that a mesh axis runs over, the one named last changes fastest.
Arguments:
- spin_state: float32 [16, 3, 16, 128, 128], P(('group', 'temp'), None, 'gz'), parts along dimension 0, may hold values from -1 to 1, as said below
- couplings: float32 [3, 32, 128, 128], P(None, ('group', 'gz')), parts along dimension 1, may hold values from -12 to 12
- inverse_temps: float32 [16], P(('group', 'temp')), parts along dimension 0, may hold values from 0.3 to 3
- colour_order: int32 [16], P(('group', 'temp')), parts along dimension 0, may hold values 0 or 1
- heat_level: float32 [16, 16, 128, 128], P(('group', 'temp'), 'gz'), parts along dimension 0, may hold values from 0.001 to 0.999
- heat_height: float32 [16, 16, 128, 128], P(('group', 'temp'), 'gz'), parts along dimension 0, may hold values from -1 to 1
- heat_angle: float32 [16, 16, 128, 128], P(('group', 'temp'), 'gz'), parts along dimension 0, may hold values from -3.140625 to 3.140625
- swap_bits: int32 [16], P(('group', 'temp')), parts along dimension 0, may hold values 0 or 1
Outputs:
- spin_final: float32 [16, 3, 16, 128, 128], P(('group', 'temp'), None, 'gz'), parts along dimension 0
- energies: float32 [16], P(('group', 'temp')), parts along dimension 0
There are 2 independent parts, one for each index of `group`. A program takes and returns all parts, laid end to end along the dimension named above; each array names one. Nothing has to cross between parts.
Inputs may be any that keep to these rules, and one draw needn't show every extreme that they name: `spin_state`: every site's three components form a vector of unit length.
All inputs are finite; a program needn't handle non-finite values. No bound on the sum of `colour_order` or of `swap_bits` on one device may be relied on, other than what follows from the above.
Results may differ from a plain program's by a relative error of at most 0.0003.
Values sent between devices are 32-bit elements; how exact they have to be, the bound alone decides.
A program may use at most 64 MiB of HBM per device.

v0:
```python
import jax
import jax.numpy as jnp
from jax import lax
from jax.sharding import PartitionSpec as P

OR_SWEEPS = 2


def passed_along(value, axis, steps):
    count = lax.axis_size(axis)
    pairs = [(source, (source + steps) % count) for source in range(count)]
    return lax.ppermute(value, axis, pairs)


def extended(array, sides, width):
    for axis, dim in sides:
        count, length = (lax.axis_size(axis), array.shape[dim])
        up = [(i, (i + 1) % count) for i in range(count)]
        down = [(j, i) for i, j in up]
        last = lax.slice_in_dim(array, length - width, length, axis=dim)
        leading = lax.slice_in_dim(array, 0, width, axis=dim)
        before = lax.ppermute(last, axis, up)
        after = lax.ppermute(leading, axis, down)
        array = jnp.concatenate([before, array, after], axis=dim)
    return array


def shifted(block, axis, distance):
    devices = range(lax.axis_size(axis))
    route = [(i - distance, i) for i in devices if i - distance in devices]
    return lax.ppermute(block, axis, route)


def reflect(current, pulled):
    projection = jnp.sum(current * pulled, axis=1, keepdims=True)
    square = jnp.sum(pulled * pulled, axis=1, keepdims=True)
    return 2.0 * projection / jnp.maximum(square, 0.01) * pulled - current


def heat_bath(pulled, beta_value, uniform_level, cosine_draw, angle_draw):
    square = jnp.sum(pulled * pulled, axis=1, keepdims=True)
    strength = jnp.sqrt(jnp.maximum(square, 0.01))
    unit_axis = pulled / strength
    reach = beta_value * strength
    cosine = 1.0 + jnp.log1p(uniform_level * jnp.expm1(-2.0 * reach)) / reach
    side = jnp.sqrt(jnp.maximum(1.0 - cosine_draw * cosine_draw, 0.0))
    proposal = jnp.concatenate(
        [side * jnp.cos(angle_draw), side * jnp.sin(angle_draw), cosine_draw], axis=1
    )
    along_axis = jnp.sum(proposal * unit_axis, axis=1, keepdims=True)
    tangent = proposal - along_axis * unit_axis
    tangent = tangent / jnp.sqrt(
        jnp.maximum(jnp.sum(tangent * tangent, axis=1, keepdims=True), 0.0001)
    )
    return cosine * unit_axis + jnp.sqrt(jnp.maximum(1.0 - cosine * cosine, 0.0)) * tangent


def local_pull(padded, bond_pad, first_plane, end_plane):
    middle = padded[:, :, first_plane:end_plane]
    east_bond = bond_pad[0, first_plane:end_plane]
    north_bond = bond_pad[1, first_plane:end_plane]
    pulled = east_bond * jnp.roll(middle, -1, 4) + jnp.roll(east_bond, 1, 2) * jnp.roll(
        middle, 1, 4
    )
    pulled = (
        pulled
        + north_bond * jnp.roll(middle, -1, 3)
        + jnp.roll(north_bond, 1, 1) * jnp.roll(middle, 1, 3)
    )
    pulled = (
        pulled + bond_pad[2, first_plane:end_plane] * padded[:, :, first_plane + 1 : end_plane + 1]
    )
    pulled = (
        pulled
        + bond_pad[2, first_plane - 1 : end_plane - 1]
        * padded[:, :, first_plane - 1 : end_plane - 1]
    )
    return (middle, pulled)


def colour_mask(colour_order, plane_start, count, row_count, column_count, colour):
    plane_index = plane_start + jnp.arange(count, dtype=jnp.int32)
    row_index = jnp.arange(row_count, dtype=jnp.int32)
    column_index = jnp.arange(column_count, dtype=jnp.int32)
    site_sum = plane_index[:, None, None] + row_index[None, :, None] + column_index[None, None, :]
    parity = (site_sum[None] + colour_order[:, None, None, None]) % 2
    return (parity == colour)[:, None]


def relax_planes(padded, bond_pad, first_plane, end_plane, chosen):
    middle, pulled = local_pull(padded, bond_pad, first_plane, end_plane)
    renewed = jnp.where(chosen, reflect(middle, pulled), middle)
    return jnp.concatenate([padded[:, :, :first_plane], renewed, padded[:, :, end_plane:]], axis=2)


def pair_swap(stacked, decisions):
    flipped = stacked[:, ::-1]
    taking = (decisions != 0).reshape((-1,) + (1,) * (stacked.ndim - 1))
    return jnp.where(taking, flipped, stacked)


def on_device(
    spin_state,
    couplings,
    inverse_temps,
    colour_order,
    heat_level,
    heat_height,
    heat_angle,
    swap_bits,
):
    replica_count, _, planes, row_count, column_count = spin_state.shape
    plane_offset = lax.axis_index("gz") * planes
    spin_now = spin_state
    lower_upward = passed_along(couplings[2:3, -1:], "gz", 1)
    lower_plane = jnp.concatenate(
        [jnp.zeros((2, 1, row_count, column_count), jnp.float32), lower_upward], axis=0
    )
    bond_near = jnp.concatenate([lower_plane, couplings], axis=1)
    for sweep_index in range(OR_SWEEPS):
        for colour in (0, 1):
            chosen = colour_mask(
                colour_order, plane_offset, planes, row_count, column_count, colour
            )
            padded = extended(spin_now, (("gz", 2),), 1)
            padded = relax_planes(padded, bond_near, 1, planes + 1, chosen)
            spin_now = padded[:, :, 1:-1]
    beta_value = inverse_temps[:, None, None, None, None]
    last_pull = None
    last_chosen = None
    for colour in (0, 1):
        chosen = colour_mask(colour_order, plane_offset, planes, row_count, column_count, colour)
        padded = extended(spin_now, (("gz", 2),), 1)
        middle, pulled = local_pull(padded, bond_near, 1, planes + 1)
        renewed = heat_bath(
            pulled, beta_value, heat_level[:, None], heat_height[:, None], heat_angle[:, None]
        )
        spin_now = jnp.where(chosen, renewed, middle)
        last_pull = pulled
        last_chosen = chosen
    site_terms = jnp.sum(spin_now * last_pull, axis=1, keepdims=True)
    local_energy = -jnp.sum(jnp.where(last_chosen, site_terms, 0.0), axis=(1, 2, 3, 4))
    total_sites = float(column_count * row_count * planes * lax.axis_size("gz"))
    energy_now = lax.psum(local_energy, "gz") / total_sites
    tail_shape = spin_now.shape[1:]
    pair_count = replica_count // 2
    spin_now = pair_swap(spin_now.reshape((pair_count, 2) + tail_shape), swap_bits[0::2]).reshape(
        spin_now.shape
    )
    energy_now = pair_swap(energy_now.reshape((pair_count, 2)), swap_bits[0::2]).reshape(
        (replica_count,)
    )
    top_send = (spin_now[-1:], energy_now[-1:], swap_bits[-1:].astype(jnp.float32))
    below_spin, below_energy, below_bit = shifted(
        (top_send[0], top_send[1], top_send[2]), "temp", 1
    )
    above_spin, above_energy = shifted((spin_now[:1], energy_now[:1]), "temp", -1)
    top_device = lax.axis_index("temp") == lax.axis_size("temp") - 1
    odd_bits = swap_bits[1::2]
    odd_bits = jnp.where((jnp.arange(pair_count) == pair_count - 1) & top_device, 0, odd_bits)
    pair_bits = jnp.concatenate([(below_bit > 0.5).astype(jnp.int32), odd_bits])
    widened = jnp.concatenate([below_spin, spin_now, above_spin], axis=0)
    widened = pair_swap(widened.reshape((pair_count + 1, 2) + tail_shape), pair_bits)
    spin_final = widened.reshape((replica_count + 2,) + tail_shape)[1:-1]
    energy_wide = jnp.concatenate([below_energy, energy_now, above_energy], axis=0)
    energy_wide = pair_swap(energy_wide.reshape((pair_count + 1, 2)), pair_bits)
    energies = energy_wide.reshape((replica_count + 2,))[1:-1]
    return (spin_final, energies)


def solution(mesh):
    return jax.shard_map(
        on_device,
        mesh=mesh,
        in_specs=(
            P(("group", "temp"), None, "gz", None, None),
            P(None, ("group", "gz"), None, None),
            P(("group", "temp")),
            P(("group", "temp")),
            P(("group", "temp"), "gz", None, None),
            P(("group", "temp"), "gz", None, None),
            P(("group", "temp"), "gz", None, None),
            P(("group", "temp")),
        ),
        out_specs=(P(("group", "temp"), None, "gz", None, None), P(("group", "temp"))),
        check_vma=False,
    )
```

profile of v0, /device:TPU:1, one launch (start us, length us, event | category | flops | bytes accessed | tf_op | source)
XLA Modules:
  0.0 188.3 jit_solution(18086211062356483955)
XLA Ops:
  0.7 1.0 slice.366
  1.6 2.1 %collective-permute-start.2 = (f32[1,1,128,128]{3,2,1,0:T(8,128)S(1)}, f32[1,1,128,128]{3,2,1,0:T(8,128)S(1)}, u32[]{:S(2)}, u32[]{:S(2)}) collective-permute-start(f32[1,1,128,128]{3,2,1,0:T(8,128)S(1)} %slice.366), channel_id=1, source_target_pairs={{0,1},{1,2},{2,3},{3,0},{4,5},{5,6},{6,7},{7,4},{8,9},{9,10},{10,1... | collective-permute-start | bytes 196616 | tf_op jit(solution)/shard_map/ppermute | solution.py:12
  3.7 2.1 %fusion.81 = (f32[2,3,1,128,128]{4,3,2,1,0:T(8,128)}, f32[2,3,1,128,128]{4,3,2,1,0:T(8,128)}) fusion(f32[2,3,4,128,128]{4,3,2,1,0:T(8,128)} %param.8), kind=kLoop, calls=%fused_computation.178 | loop fusion | bytes 1572864 | tf_op jit(solution)/shard_map/slice | solution.py:21
  5.8 2.0 %collective-permute-start.1 = (f32[2,3,1,128,128]{4,3,2,1,0:T(8,128)}, f32[2,3,1,128,128]{4,3,2,1,0:T(8,128)}, u32[]{:S(2)}, u32[]{:S(2)}) collective-permute-start(f32[2,3,1,128,128]{4,3,2,1,0:T(8,128)} %get-tuple-element.84), channel_id=1, source_target_pairs={{1,0},{2,1},{3,2},{0,3},{5,4},{6,5},{7,6},{4,7},{9,8},{10,9},{11,1... | collective-permute-start | bytes 1179656 | tf_op jit(solution)/shard_map/ppermute | solution.py:23
  7.9 0.6 fusion.83
  9.1 4.9 %collective-permute-start = (f32[1]{0:T(128)}, f32[1]{0:T(128)}, u32[]{:S(2)}, u32[]{:S(2)}) collective-permute-start(f32[1]{0:T(128)} %convert_element_type.6), channel_id=1, source_target_pairs={{0,4},{4,8},{8,12},{1,5},{5,9},{9,13},{2,6},{6,10},{10,14},{3,7},{... | collective-permute-start | bytes 20 | tf_op jit(solution)/shard_map/ppermute | solution.py:31
  14.0 2.2 %fusion.77 = (f32[2,3,4,128,127]{4,3,2,1,0:T(8,128)}, f32[2,3,4,128,127]{4,3,2,1,0:T(8,128)}) fusion(f32[2,3,4,128,128]{4,3,2,1,0:T(8,128)S(1)} %copy-done), kind=kLoop, calls=%fused_computation.174 | loop fusion | bytes 6242304 | tf_op jit(solution)/shard_map/jit(_roll_static)/slice | solution.py:62
  16.2 2.2 %fusion.78 = (f32[2,3,4,128,1]{4,3,2,1,0:T(8,128)}, f32[2,3,4,128,1]{4,3,2,1,0:T(8,128)}) fusion(f32[2,3,4,128,128]{4,3,2,1,0:T(8,128)S(1)} %copy-done), kind=kLoop, calls=%fused_computation.175 | loop fusion | bytes 49152 | tf_op jit(solution)/shard_map/jit(_roll_static)/slice | solution.py:62
  18.4 1.9 %fusion.79 = (f32[2,3,4,127,128]{4,3,2,1,0:T(8,128)}, f32[2,3,4,127,128]{4,3,2,1,0:T(8,128)}) fusion(f32[2,3,4,128,128]{4,3,2,1,0:T(8,128)S(1)} %copy-done), kind=kLoop, calls=%fused_computation.176 | loop fusion | bytes 6242304 | tf_op jit(solution)/shard_map/jit(_roll_static)/slice | solution.py:67
  21.0 3.4 %multiply_bitcast_fusion.1 = (f32[2,1,4,128,128]{4,3,2,1,0:T(8,128)S(1)}, f32[2,1,4,128,128]{4,3,2,1,0:T(8,128)S(1)}) fusion(f32[2,4,128,128]{3,2,1,0:T(8,128)} %param.14, f32[2,4,128,128]{3,2,1,0:T(8,128)S(1)} %copy-done.1), kind=kLoop, calls=%fused_computation.122 | loop fusion | flops 655360 | bytes 2097152 | tf_op jit(solution)/shard_map/mul | solution.py:48
  24.4 0.6 fusion.80
  27.1 1.4 slice_bitcast_fusion.4
  28.8 1.2 copy-done.2
  29.9 4.3 %multiply_reduce_fusion.14 = (f32[2,4,128,128]{3,2,1,0:T(8,128)S(1)}, f32[2,4,128,128]{3,2,1,0:T(8,128)S(1)}, f32[2,3,4,128,128]{4,3,2,1,0:T(8,128)S(1)}) fusion(f32[2,3,4,128,128]{4,3,2,1,0:T(8,128)S(1)} %copy-done, f32[2,3,1,128,128]{4,3,2,1,0:T(8,128)} %collective-permute-done.3, f32[4,128,128]{2,1,0:T(8,128)S(1)} %get-tuple-element.91, ...), kind=kLoop, calls=%fused_computation.104 | loop fusion | flops 7995392 | bytes 12845056 | tf_op jit(solution)/shard_map/reduce_sum | solution.py:35
  35.9 3.6 %collective-permute-start.4 = (f32[2,3,1,128,128]{4,3,2,1,0:T(8,128)S(1)}, f32[2,3,1,128,128]{4,3,2,1,0:T(8,128)S(1)}, u32[]{:S(2)}, u32[]{:S(2)}) collective-permute-start(f32[2,3,1,128,128]{4,3,2,1,0:T(8,128)S(1)} %get-tuple-element.74), channel_id=1, source_target_pairs={{1,0},{2,1},{3,2},{0,3},{5,4},{6,5},{7,6},{4,7},{9,8},{10,9},{11,1... | collective-permute-start | bytes 1179656 | tf_op jit(solution)/shard_map/ppermute | solution.py:23
  39.8 8.6 %collective-permute-done.4 = f32[2,3,1,128,128]{4,3,2,1,0:T(8,128)S(1)} collective-permute-done((f32[2,3,1,128,128]{4,3,2,1,0:T(8,128)S(1)}, f32[2,3,1,128,128]{4,3,2,1,0:T(8,128)S(1)}, u32[]{:S(2)}, u32[]{:S(2)}) %collective-permute-start.4) | collective-permute-done | bytes 393248 | tf_op jit(solution)/shard_map/ppermute | solution.py:23
  48.4 7.4 %collective-permute-done.5 = f32[2,3,1,128,128]{4,3,2,1,0:T(8,128)S(1)} collective-permute-done((f32[2,3,1,128,128]{4,3,2,1,0:T(8,128)S(1)}, f32[2,3,1,128,128]{4,3,2,1,0:T(8,128)S(1)}, u32[]{:S(2)}, u32[]{:S(2)}) %collective-permute-start.5) | collective-permute-done | bytes 393248 | tf_op jit(solution)/shard_map/ppermute | solution.py:22
  55.8 2.3 %multiply_reduce_fusion.12 = (f32[2,4,128,128]{3,2,1,0:T(8,128)S(1)}, f32[2,4,128,128]{3,2,1,0:T(8,128)S(1)}, f32[2,3,4,128,128]{4,3,2,1,0:T(8,128)S(1)}) fusion(f32[2,3,4,128,128]{4,3,2,1,0:T(8,128)S(1)} %subtract_select_fusion.3, f32[2,3,1,128,128]{4,3,2,1,0:T(8,128)S(1)} %collective-permute-done.5, f32[4,128,128]{2,1,0:T(8,128)S(1)} %get-tuple-element.91, ...), kind=kLoop, calls=%fused_computation.102 | loop fusion | flops 7995392 | bytes 12845056 | tf_op jit(solution)/shard_map/reduce_sum | solution.py:35
  59.8 1.8 collective-permute-start.6
  62.0 8.5 %collective-permute-done.6 = f32[2,3,1,128,128]{4,3,2,1,0:T(8,128)S(1)} collective-permute-done((f32[2,3,1,128,128]{4,3,2,1,0:T(8,128)S(1)}, f32[2,3,1,128,128]{4,3,2,1,0:T(8,128)S(1)}, u32[]{:S(2)}, u32[]{:S(2)}) %collective-permute-start.6) | collective-permute-done | bytes 393248 | tf_op jit(solution)/shard_map/ppermute | solution.py:23
  70.6 9.1 %collective-permute-done.7 = f32[2,3,1,128,128]{4,3,2,1,0:T(8,128)S(1)} collective-permute-done((f32[2,3,1,128,128]{4,3,2,1,0:T(8,128)S(1)}, f32[2,3,1,128,128]{4,3,2,1,0:T(8,128)S(1)}, u32[]{:S(2)}, u32[]{:S(2)}) %collective-permute-start.7) | collective-permute-done | bytes 393248 | tf_op jit(solution)/shard_map/ppermute | solution.py:22
  79.6 2.3 %multiply_reduce_fusion.10 = (f32[2,4,128,128]{3,2,1,0:T(8,128)S(1)}, f32[2,4,128,128]{3,2,1,0:T(8,128)S(1)}, f32[2,3,4,128,128]{4,3,2,1,0:T(8,128)S(1)}) fusion(f32[2,3,4,128,128]{4,3,2,1,0:T(8,128)S(1)} %subtract_select_fusion.2, f32[2,3,1,128,128]{4,3,2,1,0:T(8,128)S(1)} %collective-permute-done.7, f32[4,128,128]{2,1,0:T(8,128)S(1)} %get-tuple-element.91, ...), kind=kLoop, calls=%fused_computation.100 | loop fusion | flops 7995392 | bytes 12845056 | tf_op jit(solution)/shard_map/reduce_sum | solution.py:35
  83.6 2.3 %collective-permute-start.8 = (f32[2,3,1,128,128]{4,3,2,1,0:T(8,128)S(1)}, f32[2,3,1,128,128]{4,3,2,1,0:T(8,128)S(1)}, u32[]{:S(2)}, u32[]{:S(2)}) collective-permute-start(f32[2,3,1,128,128]{4,3,2,1,0:T(8,128)S(1)} %get-tuple-element.54), channel_id=1, source_target_pairs={{1,0},{2,1},{3,2},{0,3},{5,4},{6,5},{7,6},{4,7},{9,8},{10,9},{11,1... | collective-permute-start | bytes 1179656 | tf_op jit(solution)/shard_map/ppermute | solution.py:23
  86.2 7.8 %collective-permute-done.8 = f32[2,3,1,128,128]{4,3,2,1,0:T(8,128)S(1)} collective-permute-done((f32[2,3,1,128,128]{4,3,2,1,0:T(8,128)S(1)}, f32[2,3,1,128,128]{4,3,2,1,0:T(8,128)S(1)}, u32[]{:S(2)}, u32[]{:S(2)}) %collective-permute-start.8) | collective-permute-done | bytes 393248 | tf_op jit(solution)/shard_map/ppermute | solution.py:23
  94.0 10.4 %collective-permute-done.9 = f32[2,3,1,128,128]{4,3,2,1,0:T(8,128)S(1)} collective-permute-done((f32[2,3,1,128,128]{4,3,2,1,0:T(8,128)S(1)}, f32[2,3,1,128,128]{4,3,2,1,0:T(8,128)S(1)}, u32[]{:S(2)}, u32[]{:S(2)}) %collective-permute-start.9) | collective-permute-done | bytes 393248 | tf_op jit(solution)/shard_map/ppermute | solution.py:22
  104.4 2.3 %multiply_reduce_fusion.8 = (f32[2,4,128,128]{3,2,1,0:T(8,128)S(1)}, f32[2,4,128,128]{3,2,1,0:T(8,128)S(1)}, f32[2,3,4,128,128]{4,3,2,1,0:T(8,128)S(1)}) fusion(f32[2,3,4,128,128]{4,3,2,1,0:T(8,128)S(1)} %subtract_select_fusion.1, f32[2,3,1,128,128]{4,3,2,1,0:T(8,128)S(1)} %collective-permute-done.9, f32[4,128,128]{2,1,0:T(8,128)S(1)} %get-tuple-element.91, ...), kind=kLoop, calls=%fused_computation.98 | loop fusion | flops 7995392 | bytes 12845056 | tf_op jit(solution)/shard_map/reduce_sum | solution.py:35
  108.3 1.8 collective-permute-start.10
  110.5 7.3 %collective-permute-done.10 = f32[2,3,1,128,128]{4,3,2,1,0:T(8,128)S(1)} collective-permute-done((f32[2,3,1,128,128]{4,3,2,1,0:T(8,128)S(1)}, f32[2,3,1,128,128]{4,3,2,1,0:T(8,128)S(1)}, u32[]{:S(2)}, u32[]{:S(2)}) %collective-permute-start.10) | collective-permute-done | bytes 393248 | tf_op jit(solution)/shard_map/ppermute | solution.py:23
  117.8 9.1 %collective-permute-done.11 = f32[2,3,1,128,128]{4,3,2,1,0:T(8,128)S(1)} collective-permute-done((f32[2,3,1,128,128]{4,3,2,1,0:T(8,128)S(1)}, f32[2,3,1,128,128]{4,3,2,1,0:T(8,128)S(1)}, u32[]{:S(2)}, u32[]{:S(2)}) %collective-permute-start.11) | collective-permute-done | bytes 393248 | tf_op jit(solution)/shard_map/ppermute | solution.py:22
  127.0 2.1 %multiply_reduce_fusion.6 = (f32[2,4,128,128]{3,2,1,0:T(8,128)S(1)}, f32[2,3,4,128,128]{4,3,2,1,0:T(8,128)S(1)}) fusion(f32[2,3,4,128,128]{4,3,2,1,0:T(8,128)S(1)} %subtract_select_fusion, f32[2,3,1,128,128]{4,3,2,1,0:T(8,128)S(1)} %collective-permute-done.11, f32[4,128,128]{2,1,0:T(8,128)S(1)} %get-tuple-element.91, ...), kind=kLoop, calls=%fused_computation.96 | loop fusion | flops 7340032 | bytes 12320768 | tf_op jit(solution)/shard_map/reduce_sum | solution.py:41
  129.1 0.8 maximum_sqrt_fusion.5
  130.8 0.8 add_select_fusion.1
  132.8 1.3 collective-permute-start.12
  134.9 6.8 %collective-permute-done.12 = f32[2,3,1,128,128]{4,3,2,1,0:T(8,128)S(1)} collective-permute-done((f32[2,3,1,128,128]{4,3,2,1,0:T(8,128)S(1)}, f32[2,3,1,128,128]{4,3,2,1,0:T(8,128)S(1)}, u32[]{:S(2)}, u32[]{:S(2)}) %collective-permute-start.12) | collective-permute-done | bytes 393248 | tf_op jit(solution)/shard_map/ppermute | solution.py:23
  141.6 9.5 %collective-permute-done.13 = f32[2,3,1,128,128]{4,3,2,1,0:T(8,128)S(1)} collective-permute-done((f32[2,3,1,128,128]{4,3,2,1,0:T(8,128)S(1)}, f32[2,3,1,128,128]{4,3,2,1,0:T(8,128)S(1)}, u32[]{:S(2)}, u32[]{:S(2)}) %collective-permute-start.13) | collective-permute-done | bytes 393248 | tf_op jit(solution)/shard_map/ppermute | solution.py:22
  151.1 2.2 %multiply_reduce_fusion.3 = (f32[2,4,128,128]{3,2,1,0:T(8,128)S(1)}, f32[2,3,4,128,128]{4,3,2,1,0:T(8,128)S(1)}) fusion(f32[2,3,4,128,128]{4,3,2,1,0:T(8,128)S(1)} %add_select_fusion.1, f32[2,3,1,128,128]{4,3,2,1,0:T(8,128)S(1)} %collective-permute-done.13, f32[4,128,128]{2,1,0:T(8,128)S(1)} %get-tuple-element.91, ...), kind=kLoop, calls=%fused_computation.91 | loop fusion | flops 7340032 | bytes 12320768 | tf_op jit(solution)/shard_map/reduce_sum | solution.py:41
  153.3 0.8 maximum_sqrt_fusion.1
  155.0 0.9 multiply_reduce_fusion
  156.1 9.3 %psum.7 = f32[2]{0:T(128)S(1)} all-reduce(f32[2]{0:T(128)S(1)} %neg.3), channel_id=1, replica_groups=mesh['group'=2,'temp'=4,'gz'=4] {'gz'}, use_global_device_ids=true, to_apply=%region_16.17 | all-reduce | flops 2 | bytes 16 | tf_op jit(solution)/shard_map/psum | solution.py:144
  165.7 1.3 slice_bitcast_fusion.1
  166.9 1.9 %collective-permute-start.14 = (f32[1,3,4,128,128]{4,3,2,1,0:T(8,128)}, f32[1,3,4,128,128]{4,3,2,1,0:T(8,128)}, u32[]{:S(2)}, u32[]{:S(2)}) collective-permute-start(f32[1,3,4,128,128]{4,3,2,1,0:T(8,128)} %get-tuple-element.24), channel_id=1, source_target_pairs={{0,4},{4,8},{8,12},{1,5},{5,9},{9,13},{2,6},{6,10},{10,14},{3,7},{... | collective-permute-start | bytes 2359304 | tf_op jit(solution)/shard_map/ppermute | solution.py:31
  168.8 5.5 %collective-permute-start.15 = (f32[1,3,4,128,128]{4,3,2,1,0:T(8,128)}, f32[1,3,4,128,128]{4,3,2,1,0:T(8,128)}, u32[]{:S(2)}, u32[]{:S(2)}) collective-permute-start(f32[1,3,4,128,128]{4,3,2,1,0:T(8,128)} %get-tuple-element.25), channel_id=1, source_target_pairs={{4,0},{8,4},{12,8},{5,1},{9,5},{13,9},{6,2},{10,6},{14,10},{7,3},{... | collective-permute-start | bytes 2359304 | tf_op jit(solution)/shard_map/ppermute | solution.py:31
  174.9 1.9 %collective-permute-start.16 = (f32[1]{0:T(128)}, f32[1]{0:T(128)}, u32[]{:S(2)}, u32[]{:S(2)}) collective-permute-start(f32[1]{0:T(128)} %bitcast.16), channel_id=1, source_target_pairs={{0,4},{4,8},{8,12},{1,5},{5,9},{9,13},{2,6},{6,10},{10,14},{3,7},{... | collective-permute-start | bytes 20 | tf_op jit(solution)/shard_map/ppermute | solution.py:31
  176.8 2.9 %collective-permute-start.17 = (f32[1]{0:T(128)}, f32[1]{0:T(128)}, u32[]{:S(2)}, u32[]{:S(2)}) collective-permute-start(f32[1]{0:T(128)} %bitcast.17), channel_id=1, source_target_pairs={{4,0},{8,4},{12,8},{5,1},{9,5},{13,9},{6,2},{10,6},{14,10},{7,3},{... | collective-permute-start | bytes 20 | tf_op jit(solution)/shard_map/ppermute | solution.py:31
  179.9 2.6 %collective-permute-done.17 = f32[1]{0:T(128)} collective-permute-done((f32[1]{0:T(128)}, f32[1]{0:T(128)}, u32[]{:S(2)}, u32[]{:S(2)}) %collective-permute-start.17) | collective-permute-done | bytes 36 | tf_op jit(solution)/shard_map/ppermute | solution.py:31
  182.5 1.3 pad_maximum_fusion.17
  184.8 1.6 pad_maximum_fusion
  187.0 1.3 slice.496
  (90 shorter events, 15.2 us)
Async XLA Ops:
  0.6 13.4 %copy-start = (f32[2,3,4,128,128]{4,3,2,1,0:T(8,128)S(1)}, f32[2,3,4,128,128]{4,3,2,1,0:T(8,128)}, u32[]{:S(2)}) copy-start(f32[2,3,4,128,128]{4,3,2,1,0:T(8,128)} %param.8) | copy-start | bytes 4718596
  0.6 7.2 %copy-start.6 = (s32[2]{0:T(128)S(1)}, s32[2]{0:T(128)}, u32[]{:S(2)}) copy-start(s32[2]{0:T(128)} %param.15) | copy-start | bytes 28
  1.6 25.4 %collective-permute-start.2 = (f32[1,1,128,128]{3,2,1,0:T(8,128)S(1)}, f32[1,1,128,128]{3,2,1,0:T(8,128)S(1)}, u32[]{:S(2)}, u32[]{:S(2)}) collective-permute-start(f32[1,1,128,128]{3,2,1,0:T(8,128)S(1)} %slice.366), channel_id=1, source_target_pairs={{0,1},{1,2},{2,3},{3,0},{4,5},{5,6},{6,7},{7,4},{8,9},{9,10},{10,1... | collective-permute-start | bytes 196616 | tf_op jit(solution)/shard_map/ppermute | solution.py:12
  5.8 22.9 %collective-permute-start.1 = (f32[2,3,1,128,128]{4,3,2,1,0:T(8,128)}, f32[2,3,1,128,128]{4,3,2,1,0:T(8,128)}, u32[]{:S(2)}, u32[]{:S(2)}) collective-permute-start(f32[2,3,1,128,128]{4,3,2,1,0:T(8,128)} %get-tuple-element.84), channel_id=1, source_target_pairs={{1,0},{2,1},{3,2},{0,3},{5,4},{6,5},{7,6},{4,7},{9,8},{10,9},{11,1... | collective-permute-start | bytes 1179656 | tf_op jit(solution)/shard_map/ppermute | solution.py:23
  7.9 20.9 %collective-permute-start.3 = (f32[2,3,1,128,128]{4,3,2,1,0:T(8,128)}, f32[2,3,1,128,128]{4,3,2,1,0:T(8,128)}, u32[]{:S(2)}, u32[]{:S(2)}) collective-permute-start(f32[2,3,1,128,128]{4,3,2,1,0:T(8,128)} %get-tuple-element.85), channel_id=1, source_target_pairs={{0,1},{1,2},{2,3},{3,0},{4,5},{5,6},{6,7},{7,4},{8,9},{9,10},{10,1... | collective-permute-start | bytes 1179656 | tf_op jit(solution)/shard_map/ppermute | solution.py:22
  9.1 17.3 %collective-permute-start = (f32[1]{0:T(128)}, f32[1]{0:T(128)}, u32[]{:S(2)}, u32[]{:S(2)}) collective-permute-start(f32[1]{0:T(128)} %convert_element_type.6), channel_id=1, source_target_pairs={{0,4},{4,8},{8,12},{1,5},{5,9},{9,13},{2,6},{6,10},{10,14},{3,7},{... | collective-permute-start | bytes 20 | tf_op jit(solution)/shard_map/ppermute | solution.py:31
  18.4 2.2 %copy-start.8 = (s32[2]{0:T(128)S(1)}, s32[2]{0:T(128)}, u32[]{:S(2)}) copy-start(s32[2]{0:T(128)} %param.11) | copy-start | bytes 28
  18.4 2.6 %copy-start.1 = (f32[2,4,128,128]{3,2,1,0:T(8,128)S(1)}, f32[2,4,128,128]{3,2,1,0:T(8,128)}, u32[]{:S(2)}) copy-start(f32[2,4,128,128]{3,2,1,0:T(8,128)} %param.13) | copy-start | bytes 1572868
  27.1 1.7 copy-start.3
  28.4 1.5 copy-start.2
  28.4 1.5 copy-start.5
  35.9 12.5 %collective-permute-start.4 = (f32[2,3,1,128,128]{4,3,2,1,0:T(8,128)S(1)}, f32[2,3,1,128,128]{4,3,2,1,0:T(8,128)S(1)}, u32[]{:S(2)}, u32[]{:S(2)}) collective-permute-start(f32[2,3,1,128,128]{4,3,2,1,0:T(8,128)S(1)} %get-tuple-element.74), channel_id=1, source_target_pairs={{1,0},{2,1},{3,2},{0,3},{5,4},{6,5},{7,6},{4,7},{9,8},{10,9},{11,1... | collective-permute-start | bytes 1179656 | tf_op jit(solution)/shard_map/ppermute | solution.py:23
  39.5 16.4 %collective-permute-start.5 = (f32[2,3,1,128,128]{4,3,2,1,0:T(8,128)S(1)}, f32[2,3,1,128,128]{4,3,2,1,0:T(8,128)S(1)}, u32[]{:S(2)}, u32[]{:S(2)}) collective-permute-start(f32[2,3,1,128,128]{4,3,2,1,0:T(8,128)S(1)} %get-tuple-element.75), channel_id=1, source_target_pairs={{0,1},{1,2},{2,3},{3,0},{4,5},{5,6},{6,7},{7,4},{8,9},{9,10},{10,1... | collective-permute-start | bytes 1179656 | tf_op jit(solution)/shard_map/ppermute | solution.py:22
  59.8 10.8 %collective-permute-start.6 = (f32[2,3,1,128,128]{4,3,2,1,0:T(8,128)S(1)}, f32[2,3,1,128,128]{4,3,2,1,0:T(8,128)S(1)}, u32[]{:S(2)}, u32[]{:S(2)}) collective-permute-start(f32[2,3,1,128,128]{4,3,2,1,0:T(8,128)S(1)} %get-tuple-element.64), channel_id=1, source_target_pairs={{1,0},{2,1},{3,2},{0,3},{5,4},{6,5},{7,6},{4,7},{9,8},{10,9},{11,1... | collective-permute-start | bytes 1179656 | tf_op jit(solution)/shard_map/ppermute | solution.py:23
  61.6 18.0 %collective-permute-start.7 = (f32[2,3,1,128,128]{4,3,2,1,0:T(8,128)S(1)}, f32[2,3,1,128,128]{4,3,2,1,0:T(8,128)S(1)}, u32[]{:S(2)}, u32[]{:S(2)}) collective-permute-start(f32[2,3,1,128,128]{4,3,2,1,0:T(8,128)S(1)} %get-tuple-element.65), channel_id=1, source_target_pairs={{0,1},{1,2},{2,3},{3,0},{4,5},{5,6},{6,7},{7,4},{8,9},{9,10},{10,1... | collective-permute-start | bytes 1179656 | tf_op jit(solution)/shard_map/ppermute | solution.py:22
  83.6 10.4 %collective-permute-start.8 = (f32[2,3,1,128,128]{4,3,2,1,0:T(8,128)S(1)}, f32[2,3,1,128,128]{4,3,2,1,0:T(8,128)S(1)}, u32[]{:S(2)}, u32[]{:S(2)}) collective-permute-start(f32[2,3,1,128,128]{4,3,2,1,0:T(8,128)S(1)} %get-tuple-element.54), channel_id=1, source_target_pairs={{1,0},{2,1},{3,2},{0,3},{5,4},{6,5},{7,6},{4,7},{9,8},{10,9},{11,1... | collective-permute-start | bytes 1179656 | tf_op jit(solution)/shard_map/ppermute | solution.py:23
  85.9 18.5 %collective-permute-start.9 = (f32[2,3,1,128,128]{4,3,2,1,0:T(8,128)S(1)}, f32[2,3,1,128,128]{4,3,2,1,0:T(8,128)S(1)}, u32[]{:S(2)}, u32[]{:S(2)}) collective-permute-start(f32[2,3,1,128,128]{4,3,2,1,0:T(8,128)S(1)} %get-tuple-element.55), channel_id=1, source_target_pairs={{0,1},{1,2},{2,3},{3,0},{4,5},{5,6},{6,7},{7,4},{8,9},{9,10},{10,1... | collective-permute-start | bytes 1179656 | tf_op jit(solution)/shard_map/ppermute | solution.py:22
  108.3 9.5 %collective-permute-start.10 = (f32[2,3,1,128,128]{4,3,2,1,0:T(8,128)S(1)}, f32[2,3,1,128,128]{4,3,2,1,0:T(8,128)S(1)}, u32[]{:S(2)}, u32[]{:S(2)}) collective-permute-start(f32[2,3,1,128,128]{4,3,2,1,0:T(8,128)S(1)} %get-tuple-element.44), channel_id=1, source_target_pairs={{1,0},{2,1},{3,2},{0,3},{5,4},{6,5},{7,6},{4,7},{9,8},{10,9},{11,1... | collective-permute-start | bytes 1179656 | tf_op jit(solution)/shard_map/ppermute | solution.py:23
  110.1 16.8 %collective-permute-start.11 = (f32[2,3,1,128,128]{4,3,2,1,0:T(8,128)S(1)}, f32[2,3,1,128,128]{4,3,2,1,0:T(8,128)S(1)}, u32[]{:S(2)}, u32[]{:S(2)}) collective-permute-start(f32[2,3,1,128,128]{4,3,2,1,0:T(8,128)S(1)} %get-tuple-element.45), channel_id=1, source_target_pairs={{0,1},{1,2},{2,3},{3,0},{4,5},{5,6},{6,7},{7,4},{8,9},{9,10},{10,1... | collective-permute-start | bytes 1179656 | tf_op jit(solution)/shard_map/ppermute | solution.py:22
  127.0 2.1 %copy-start.4 = (f32[2,4,128,128]{3,2,1,0:T(8,128)S(1)}, f32[2,4,128,128]{3,2,1,0:T(8,128)}, u32[]{:S(2)}) copy-start(f32[2,4,128,128]{3,2,1,0:T(8,128)} %param.12) | copy-start | bytes 1572868
  127.0 2.2 %copy-start.7 = (f32[2]{0:T(128)S(1)}, f32[2]{0:T(128)}, u32[]{:S(2)}) copy-start(f32[2]{0:T(128)} %param.10) | copy-start | bytes 28
  132.8 8.8 %collective-permute-start.12 = (f32[2,3,1,128,128]{4,3,2,1,0:T(8,128)S(1)}, f32[2,3,1,128,128]{4,3,2,1,0:T(8,128)S(1)}, u32[]{:S(2)}, u32[]{:S(2)}) collective-permute-start(f32[2,3,1,128,128]{4,3,2,1,0:T(8,128)S(1)} %get-tuple-element.34), channel_id=1, source_target_pairs={{1,0},{2,1},{3,2},{0,3},{5,4},{6,5},{7,6},{4,7},{9,8},{10,9},{11,1... | collective-permute-start | bytes 1179656 | tf_op jit(solution)/shard_map/ppermute | solution.py:23
  134.1 17.0 %collective-permute-start.13 = (f32[2,3,1,128,128]{4,3,2,1,0:T(8,128)S(1)}, f32[2,3,1,128,128]{4,3,2,1,0:T(8,128)S(1)}, u32[]{:S(2)}, u32[]{:S(2)}) collective-permute-start(f32[2,3,1,128,128]{4,3,2,1,0:T(8,128)S(1)} %get-tuple-element.35), channel_id=1, source_target_pairs={{0,1},{1,2},{2,3},{3,0},{4,5},{5,6},{6,7},{7,4},{8,9},{9,10},{10,1... | collective-permute-start | bytes 1179656 | tf_op jit(solution)/shard_map/ppermute | solution.py:22
  166.9 17.9 %collective-permute-start.14 = (f32[1,3,4,128,128]{4,3,2,1,0:T(8,128)}, f32[1,3,4,128,128]{4,3,2,1,0:T(8,128)}, u32[]{:S(2)}, u32[]{:S(2)}) collective-permute-start(f32[1,3,4,128,128]{4,3,2,1,0:T(8,128)} %get-tuple-element.24), channel_id=1, source_target_pairs={{0,4},{4,8},{8,12},{1,5},{5,9},{9,13},{2,6},{6,10},{10,14},{3,7},{... | collective-permute-start | bytes 2359304 | tf_op jit(solution)/shard_map/ppermute | solution.py:31
  168.8 16.0 %collective-permute-start.15 = (f32[1,3,4,128,128]{4,3,2,1,0:T(8,128)}, f32[1,3,4,128,128]{4,3,2,1,0:T(8,128)}, u32[]{:S(2)}, u32[]{:S(2)}) collective-permute-start(f32[1,3,4,128,128]{4,3,2,1,0:T(8,128)} %get-tuple-element.25), channel_id=1, source_target_pairs={{4,0},{8,4},{12,8},{5,1},{9,5},{13,9},{6,2},{10,6},{14,10},{7,3},{... | collective-permute-start | bytes 2359304 | tf_op jit(solution)/shard_map/ppermute | solution.py:31
  174.9 5.0 %collective-permute-start.16 = (f32[1]{0:T(128)}, f32[1]{0:T(128)}, u32[]{:S(2)}, u32[]{:S(2)}) collective-permute-start(f32[1]{0:T(128)} %bitcast.16), channel_id=1, source_target_pairs={{0,4},{4,8},{8,12},{1,5},{5,9},{9,13},{2,6},{6,10},{10,14},{3,7},{... | collective-permute-start | bytes 20 | tf_op jit(solution)/shard_map/ppermute | solution.py:31
  176.8 5.7 %collective-permute-start.17 = (f32[1]{0:T(128)}, f32[1]{0:T(128)}, u32[]{:S(2)}, u32[]{:S(2)}) collective-permute-start(f32[1]{0:T(128)} %bitcast.17), channel_id=1, source_target_pairs={{4,0},{8,4},{12,8},{5,1},{9,5},{13,9},{6,2},{10,6},{14,10},{7,3},{... | collective-permute-start | bytes 20 | tf_op jit(solution)/shard_map/ppermute | solution.py:31
where the time goes:
time: 189 us; the launch traced here: 188 us
  waiting for transfers between devices  87.1 us (46%)
  starting transfers between devices  32.4 us (17%)
  other arithmetic  32 us (17%)
  local copies, waits for them, and re-layouts  23.6 us (12%)
  blocking collectives  9.26 us (5%)
  between operations  3.85 us (2%)
    ppermute x6, waiting for transfers between devices, extended(): before = lax.ppermute(last, axis, up)  45.5 us
    ppermute x6, waiting for transfers between devices, extended(): after = lax.ppermute(leading, axis, down)  38.9 us
    ppermute x5, starting transfers between devices, shifted(): return lax.ppermute(block, axis, route)  17.1 us
    ppermute x6, starting transfers between devices, extended(): after = lax.ppermute(leading, axis, down)  12.8 us
    reduce_sum x4, other arithmetic, reflect(): projection = jnp.sum(current * pulled, axis=1, keepdims=True)  11.3 us
    slice x12, local copies, waits for them, and re-layouts, local_pull(): jnp.roll(middle, -1, 4)  9.94 us
    psum x1, blocking collectives, on_device(): energy_now = lax.psum(local_energy, 'gz') / total_sites  9.26 us
    slice x12, local copies, waits for them, and re-layouts, local_pull(): jnp.roll(middle, -1, 3)  4.39 us
  transfers between devices with their start and end apart: 18, of which 11 were waited for; matrix products, arithmetic and copies ran while one was open for 11% of the time, Pallas kernels for 0%

commit v1 on v0

v1 whole, which is shorter than its diff:
```python
import functools
import math

import jax
import jax.numpy as jnp
from jax import lax
from jax.experimental import pallas as pl
from jax.experimental.pallas import tpu as pltpu
from jax.sharding import PartitionSpec as P

OR_SWEEPS = 2
HALVES = 2 * OR_SWEEPS + 2
PAD = 8
MESH = pl.DeviceIdType.MESH
SIN_TERMS = [(-1.0) ** i / math.factorial(2 * i + 1) for i in range(8)]
COS_TERMS = [(-1.0) ** i / math.factorial(2 * i) for i in range(9)]


def horner(terms, value):
    total = jnp.full_like(value, terms[-1])
    for term in terms[-2::-1]:
        total = total * value + term
    return total


def cos_sin(angle):
    half = 0.5 * angle
    square = half * half
    sine = half * horner(SIN_TERMS, square)
    cosine = horner(COS_TERMS, square)
    return 1.0 - 2.0 * sine * sine, 2.0 * sine * cosine


def dot3(a, b):
    return a[0] * b[0] + a[1] * b[1] + a[2] * b[2]


def reflect(current, pulled):
    factor = 2.0 * dot3(current, pulled) / jnp.maximum(dot3(pulled, pulled), 0.01)
    return [factor * p - s for p, s in zip(pulled, current)]


def heat_bath(pulled, beta, level, trial):
    strength = jnp.sqrt(jnp.maximum(dot3(pulled, pulled), 0.01))
    inverse = 1.0 / strength
    axis = [p * inverse for p in pulled]
    reach = beta * strength
    shrink = -jnp.tanh(reach) * (jnp.exp(-2.0 * reach) + 1.0)
    cosine = 1.0 + jnp.log1p(level * shrink) / reach
    along = dot3(trial, axis)
    tangent = [t - along * a for t, a in zip(trial, axis)]
    scale = jnp.sqrt(jnp.maximum(1.0 - cosine * cosine, 0.0)) * (
        1.0 / jnp.sqrt(jnp.maximum(dot3(tangent, tangent), 0.0001))
    )
    return [cosine * a + scale * t for a, t in zip(axis, tangent)]


def kernel(
    dims,
    spin_hbm,
    coup_hbm,
    beta_ref,
    order_ref,
    level_hbm,
    height_hbm,
    angle_hbm,
    bits_ref,
    out_ref,
    eout_ref,
    spin_in,
    coup_in,
    level_in,
    height_in,
    angle_in,
    below_bond,
    sp,
    xo,
    xr,
    yi,
    yo,
    zu,
    zd,
    lv,
    ut,
    eacc,
    ebuf,
    tsend,
    trecv,
    rbuf,
    in_sem,
    bond_sem,
    hsend,
    hrecv,
    esend,
    erecv,
    tssem,
    trsem,
    xsend,
    xrecv,
):
    count, planes, rows, width, n, m = dims
    k = rows // 2
    chunk = 32 if k % 32 == 0 else 8
    g = lax.axis_index("gz")
    t = lax.axis_index("temp")
    up, down = lax.rem(g + 1, n), lax.rem(g + n - 1, n)
    has_below, has_above = t > 0, t < m - 1

    loads = [
        pltpu.make_async_copy(src, dst, in_sem.at[i])
        for i, (src, dst) in enumerate(
            (
                (spin_hbm, spin_in),
                (coup_hbm, coup_in),
                (level_hbm, level_in),
                (height_hbm, height_in),
                (angle_hbm, angle_in),
            )
        )
    ]
    for load in loads:
        load.start()

    barrier = pltpu.get_barrier_semaphore()
    for d in range(1, n):
        pl.semaphore_signal(
            barrier, inc=1, device_id={"gz": lax.rem(g + d, n)}, device_id_type=MESH
        )

    @pl.when(has_below)
    def _():
        pl.semaphore_signal(barrier, inc=1, device_id={"temp": t - 1}, device_id_type=MESH)

    @pl.when(has_above)
    def _():
        pl.semaphore_signal(barrier, inc=1, device_id={"temp": t + 1}, device_id_type=MESH)

    pl.semaphore_wait(barrier, n - 1 + has_below.astype(jnp.int32) + has_above.astype(jnp.int32))

    def parity(r, z, size):
        lane = lax.broadcasted_iota(jnp.int32, (size, width), 1)
        return ((lane + (g * planes + z + order_ref[r])) & 1) != 0

    def halves(ref, index, start, size):
        even = ref[index + (pl.ds(2 * start, size, stride=2), slice(None))]
        odd = ref[index + (pl.ds(2 * start + 1, size, stride=2), slice(None))]
        return even, odd

    def put_spin(c, r, d, z, start, value):
        size = value.shape[0]
        sp[c, r, d, z + 1, pl.ds(PAD + start, size), :] = value
        if start == 0:
            sp[c, r, d, z + 1, pl.ds(PAD + k, 1), :] = value[0:1]
        if start + size == k:
            sp[c, r, d, z + 1, pl.ds(PAD - 1, 1), :] = value[size - 1 : size]

    def pack_spin(r, z):
        e = parity(r, z, k)
        for d in range(3):
            even, odd = halves(spin_in, (r, d, z), 0, k)
            put_spin(0, r, d, z, 0, jnp.where(e, odd, even))
            put_spin(1, r, d, z, 0, jnp.where(e, even, odd))

    def halo(x, r, side):
        c = 1 - x % 2
        source, target = (1, planes + 1) if side == 0 else (planes, 0)
        return pltpu.make_async_remote_copy(
            src_ref=sp.at[c, r, :, source, pl.ds(PAD, k), :],
            dst_ref=sp.at[c, r, :, target, pl.ds(PAD, k), :],
            send_sem=hsend.at[x, r, side],
            recv_sem=hrecv.at[x, r, side],
            device_id={"gz": down if side == 0 else up},
            device_id_type=MESH,
        )

    def edges(r, action):
        def step(i, carry):
            action(r, i * (planes - 1))
            return carry

        lax.fori_loop(0, 2, step, 0)

    def inner(action):
        def step(i, carry):
            action(i // (planes - 2), 1 + i % (planes - 2))
            return carry

        if planes > 2:
            lax.fori_loop(0, count * (planes - 2), step, 0)

    loads[0].wait()
    for r in range(count):
        edges(r, pack_spin)
        for side in (0, 1):
            halo(0, r, side).start()
    loads[1].wait()
    bond = pltpu.make_async_remote_copy(
        src_ref=coup_in.at[2, planes - 1],
        dst_ref=below_bond,
        send_sem=bond_sem.at[0],
        recv_sem=bond_sem.at[1],
        device_id={"gz": up},
        device_id_type=MESH,
    )
    bond.start()
    inner(pack_spin)

    def pack_bonds(i, carry):
        r, z = i // planes, i % planes
        e = parity(r, z, k)
        even, odd = halves(coup_in, (0, z), 0, k)
        first, second = jnp.where(e, odd, even), jnp.where(e, even, odd)
        xo[0, r, z] = first
        xo[1, r, z] = second
        xr[0, r, z] = pltpu.roll(second, 1, 1)
        xr[1, r, z] = pltpu.roll(first, 1, 1)
        even, odd = halves(coup_in, (1, z), 0, k)
        before = pltpu.roll(odd, 1, 0)
        yi[r, z] = even
        yo[0, r, z] = jnp.where(e, odd, before)
        yo[1, r, z] = jnp.where(e, before, odd)
        even, odd = halves(coup_in, (2, z), 0, k)
        zu[0, r, z] = jnp.where(e, odd, even)
        zu[1, r, z] = jnp.where(e, even, odd)
        return carry

    def pack_lower(i, carry):
        r, z = i // (planes - 1), 1 + i % (planes - 1)
        e = parity(r, z, k)
        even, odd = halves(coup_in, (2, z - 1), 0, k)
        zd[0, r, z] = jnp.where(e, odd, even)
        zd[1, r, z] = jnp.where(e, even, odd)
        return carry

    lax.fori_loop(0, count * planes, pack_bonds, 0)
    lax.fori_loop(0, count * (planes - 1), pack_lower, 0)
    bond.wait()
    for r in range(count):
        e = parity(r, 0, k)
        even, odd = halves(below_bond, (), 0, k)
        zd[0, r, 0] = jnp.where(e, odd, even)
        zd[1, r, 0] = jnp.where(e, even, odd)

    def pull(c, r, z, start):
        o = 1 - c
        part = pl.ds(start, chunk)
        e = parity(r, z, chunk)
        bx, br, by = xo[c, r, z, part, :], xr[c, r, z, part, :], yi[r, z, part, :]
        bo, bu, bd = yo[c, r, z, part, :], zu[c, r, z, part, :], zd[c, r, z, part, :]
        pulled = []
        for d in range(3):
            mid = sp[o, r, d, z + 1, pl.ds(PAD + start, chunk), :]
            nxt = sp[o, r, d, z + 1, pl.ds(PAD + start + 1, chunk), :]
            prv = sp[o, r, d, z + 1, pl.ds(PAD + start - 1, chunk), :]
            outer = jnp.where(e, nxt, prv) if c == 0 else jnp.where(e, prv, nxt)
            total = bx * pltpu.roll(mid, width - 1, 1) + br * pltpu.roll(mid, 1, 1)
            total = total + by * mid + bo * outer
            total = total + bu * sp[o, r, d, z + 2, pl.ds(PAD + start, chunk), :]
            total = total + bd * sp[o, r, d, z, pl.ds(PAD + start, chunk), :]
            pulled.append(total)
        return pulled

    def relax(c, r, z):
        for start in range(0, k, chunk):
            pulled = pull(c, r, z, start)
            current = [sp[c, r, d, z + 1, pl.ds(PAD + start, chunk), :] for d in range(3)]
            for d, value in enumerate(reflect(current, pulled)):
                put_spin(c, r, d, z, start, value)

    def heat(c, r, z):
        for start in range(0, k, chunk):
            part = pl.ds(start, chunk)
            pulled = pull(c, r, z, start)
            trial = [ut[c, r, d, z, part, :] for d in range(3)]
            renewed = heat_bath(pulled, beta_ref[r], lv[c, r, z, part, :], trial)
            for d, value in enumerate(renewed):
                put_spin(c, r, d, z, start, value)
            if c == 1:
                terms = dot3(renewed, pulled)
                eacc[r] = eacc[r] + sum(terms[j : j + 8] for j in range(0, chunk, 8))

    def pack_heat(r):
        def step(z, carry):
            for start in range(0, k, chunk):
                part = pl.ds(start, chunk)
                e = parity(r, z, chunk)
                even, odd = halves(level_in, (r, z), start, chunk)
                lv[0, r, z, part, :] = jnp.where(e, odd, even)
                lv[1, r, z, part, :] = jnp.where(e, even, odd)
                angles = halves(angle_in, (r, z), start, chunk)
                heights = halves(height_in, (r, z), start, chunk)
                trials = []
                for angle, height in zip(angles, heights):
                    side = jnp.sqrt(jnp.maximum(1.0 - height * height, 0.0))
                    cosine, sine = cos_sin(angle)
                    trials.append((side * cosine, side * sine, height))
                for d in range(3):
                    ut[0, r, d, z, part, :] = jnp.where(e, trials[1][d], trials[0][d])
                    ut[1, r, d, z, part, :] = jnp.where(e, trials[0][d], trials[1][d])
            return carry

        lax.fori_loop(0, planes, step, 0)

    def take_halo(x, r):
        for side in (0, 1):
            halo(x, r, side).wait_recv()
            if x >= 1:
                halo(x - 1, r, side).wait_send()

    eacc[...] = jnp.zeros_like(eacc)
    for x in range(HALVES - 1):
        c = x % 2
        work = functools.partial(relax if x < 2 * OR_SWEEPS else heat, c)
        for r in range(count):
            take_halo(x, r)
            edges(r, work)
            for side in (0, 1):
                halo(x + 1, r, side).start()
        inner(work)
        if x == 0:
            for load in loads[2:]:
                load.wait()
        for r in range(count):
            if r % (2 * OR_SWEEPS) == x:
                pack_heat(r)

    def flag(j, size):
        return jnp.full((size, width), bits_ref[j], jnp.int32) != 0

    def unpack(z):
        for r in range(0, count, 2):
            taking = flag(r, k)
            masks = [parity(r + j, z, k) for j in (0, 1)]
            for d in range(3):
                both = []
                for j in (0, 1):
                    first = sp[0, r + j, d, z + 1, pl.ds(PAD, k), :]
                    second = sp[1, r + j, d, z + 1, pl.ds(PAD, k), :]
                    both.append(
                        (jnp.where(masks[j], second, first), jnp.where(masks[j], first, second))
                    )
                for row in (0, 1):
                    low, top = both[0][row], both[1][row]
                    place = pl.ds(row, k, stride=2)
                    out_ref[r, d, z, place, :] = jnp.where(taking, top, low)
                    out_ref[r + 1, d, z, place, :] = jnp.where(taking, low, top)

    def ship(z, side):
        return pltpu.make_async_remote_copy(
            src_ref=out_ref.at[count - 1 if side == 0 else 0, :, z],
            dst_ref=rbuf.at[side, :, z],
            send_sem=xsend.at[z, side],
            recv_sem=xrecv.at[z, side],
            device_id={"temp": t + 1 if side == 0 else t - 1},
            device_id_type=MESH,
        )

    def finish(plane_list):
        for z in plane_list:
            unpack(z)

            @pl.when(has_above)
            def _():
                ship(z, 0).start()

            @pl.when(has_below)
            def _():
                ship(z, 1).start()

    x = HALVES - 1
    work = functools.partial(heat, 1)
    inner(work)
    middle = list(range(1, planes - 1))
    outside = [0, planes - 1]
    finish(middle)
    for r in range(count):
        take_halo(x, r)
        edges(r, work)
    swaps = []
    for d in range(1, n):
        swaps.append(
            pltpu.make_async_remote_copy(
                src_ref=eacc,
                dst_ref=ebuf.at[d - 1],
                send_sem=esend.at[d - 1],
                recv_sem=erecv.at[d - 1],
                device_id={"gz": lax.rem(g + d, n)},
                device_id_type=MESH,
            )
        )
    for swap in swaps:
        swap.start()
    finish(outside)

    for swap in swaps:
        swap.wait()
    sites = float(width * rows * planes * n)
    energy = []
    for r in range(count):
        total = eacc[r]
        for d in range(n - 1):
            total = total + ebuf[d, r]
        summed = jnp.sum(jnp.sum(total, axis=0, keepdims=True), axis=1, keepdims=True)
        energy.append(jnp.broadcast_to(-summed / sites, (8, width)))
    for r in range(0, count, 2):
        taking = flag(r, 8)
        low, top = energy[r], energy[r + 1]
        energy[r], energy[r + 1] = jnp.where(taking, top, low), jnp.where(taking, low, top)
    tsend[0] = energy[count - 1]
    tsend[1] = jnp.full((8, width), bits_ref[count - 1], jnp.int32).astype(jnp.float32)
    tsend[2] = energy[0]

    def tell(side):
        part = pl.ds(0, 2) if side == 0 else pl.ds(2, 1)
        return pltpu.make_async_remote_copy(
            src_ref=tsend.at[part],
            dst_ref=trecv.at[part],
            send_sem=tssem.at[side],
            recv_sem=trsem.at[side],
            device_id={"temp": t + 1 if side == 0 else t - 1},
            device_id_type=MESH,
        )

    @pl.when(has_above)
    def _():
        tell(0).start()

    @pl.when(has_below)
    def _():
        tell(1).start()

    for r in range(1, count - 1, 2):
        taking = flag(r, 8)
        low, top = energy[r], energy[r + 1]
        energy[r], energy[r + 1] = jnp.where(taking, top, low), jnp.where(taking, low, top)
        wide = flag(r, rows)

        def exchange(i, carry):
            d, z = i // planes, i % planes
            a, b = out_ref[r, d, z], out_ref[r + 1, d, z]
            out_ref[r, d, z] = jnp.where(wide, b, a)
            out_ref[r + 1, d, z] = jnp.where(wide, a, b)
            return carry

        lax.fori_loop(0, 3 * planes, exchange, 0)

    for r in range(count):
        eout_ref[r] = jnp.max(energy[r])

    for r in range(count):
        for side in (0, 1):
            halo(x, r, side).wait_send()

    @pl.when(has_above)
    def _():
        tell(0).wait_send()
        tell(1).wait_recv()
        wide = flag(count - 1, rows)
        eout_ref[count - 1] = jnp.max(
            jnp.where(flag(count - 1, 8), trecv[2], energy[count - 1])
        )
        for z in middle + outside:
            ship(z, 0).wait_send()
            ship(z, 1).wait_recv()
            for d in range(3):
                out_ref[count - 1, d, z] = jnp.where(wide, rbuf[1, d, z], out_ref[count - 1, d, z])

    @pl.when(has_below)
    def _():
        tell(1).wait_send()
        tell(0).wait_recv()
        eout_ref[0] = jnp.max(jnp.where(trecv[1] > 0.5, trecv[0], energy[0]))
        wide = jnp.broadcast_to(trecv[1][0:1], (rows, width)) > 0.5
        for z in middle + outside:
            ship(z, 1).wait_send()
            ship(z, 0).wait_recv()
            for d in range(3):
                out_ref[0, d, z] = jnp.where(wide, rbuf[0, d, z], out_ref[0, d, z])


def on_device(n, m, spin, coup, beta, order, level, height, angle, bits):
    count, _, planes, rows, width = spin.shape
    k = rows // 2
    f32 = jnp.float32
    hbm = pl.BlockSpec(memory_space=pltpu.HBM)
    smem = pl.BlockSpec(memory_space=pltpu.SMEM)
    dma = pltpu.SemaphoreType.DMA
    bonds = pltpu.VMEM((2, count, planes, k, width), f32)
    return pl.pallas_call(
        functools.partial(kernel, (count, planes, rows, width, n, m)),
        out_shape=(
            jax.ShapeDtypeStruct(spin.shape, f32),
            jax.ShapeDtypeStruct((count,), f32),
        ),
        in_specs=[hbm, hbm, smem, smem, hbm, hbm, hbm, smem],
        out_specs=(pl.BlockSpec(memory_space=pltpu.VMEM), smem),
        scratch_shapes=[
            pltpu.VMEM(spin.shape, f32),
            pltpu.VMEM(coup.shape, f32),
            pltpu.VMEM(level.shape, f32),
            pltpu.VMEM(level.shape, f32),
            pltpu.VMEM(level.shape, f32),
            pltpu.VMEM((rows, width), f32),
            pltpu.VMEM((2, count, 3, planes + 2, k + 2 * PAD, width), f32),
            bonds,
            bonds,
            pltpu.VMEM((count, planes, k, width), f32),
            bonds,
            bonds,
            bonds,
            bonds,
            pltpu.VMEM((2, count, 3, planes, k, width), f32),
            pltpu.VMEM((count, 8, width), f32),
            pltpu.VMEM((n - 1, count, 8, width), f32),
            pltpu.VMEM((3, 8, width), f32),
            pltpu.VMEM((3, 8, width), f32),
            pltpu.VMEM((2, 3, planes, rows, width), f32),
            dma((5,)),
            dma((2,)),
            dma((HALVES, count, 2)),
            dma((HALVES, count, 2)),
            dma((n - 1,)),
            dma((n - 1,)),
            dma((2,)),
            dma((2,)),
            dma((planes, 2)),
            dma((planes, 2)),
        ],
        compiler_params=pltpu.CompilerParams(
            collective_id=0, has_side_effects=True, vmem_limit_bytes=48 * 1024 * 1024
        ),
    )(spin, coup, beta, order, level, height, angle, bits)


def solution(mesh):
    n, m = mesh.shape["gz"], mesh.shape["temp"]
    return jax.shard_map(
        functools.partial(on_device, n, m),
        mesh=mesh,
        in_specs=(
            P(("group", "temp"), None, "gz", None, None),
            P(None, ("group", "gz"), None, None),
            P(("group", "temp")),
            P(("group", "temp")),
            P(("group", "temp"), "gz", None, None),
            P(("group", "temp"), "gz", None, None),
            P(("group", "temp"), "gz", None, None),
            P(("group", "temp")),
        ),
        out_specs=(P(("group", "temp"), None, "gz", None, None), P(("group", "temp"))),
        check_vma=False,
    )
```

time: 189 us -> 79.9 us (0.42)
  waiting for transfers between devices: 87.1 us -> 0 us
  Pallas kernels: 0 us -> 69.6 us
  starting transfers between devices: 32.4 us -> 0 us
  other arithmetic: 32 us -> 0 us
  local copies, waits for them, and re-layouts: 23.6 us -> 9.28 us
  blocking collectives: 9.26 us -> 0 us
  between operations: 3.85 us -> 0.66 us
    ppermute x18 -> x0, waiting for transfers between devices: 87.1 us -> none  [the longest x6 45.5 us: extended(): before = lax.ppermute(last, axis, up)]
    pallas_call x0 -> x1, Pallas kernels: none -> 69.6 us  [on_device(): pl.pallas_call(functools.partial(kernel, (count, planes, rows, width, n,...]
    ppermute x18 -> x0, starting transfers between devices: 32.4 us -> none  [the longest x5 17.1 us: shifted(): return lax.ppermute(block, axis, route)]
    slice x38 -> x0, local copies, waits for them, and re-layouts: 22.1 us -> none  [the longest x12 9.94 us: local_pull(): jnp.roll(middle, -1, 4)]
    reduce_sum x12 -> x0, other arithmetic: 18.2 us -> none  [the longest x4 11.3 us: reflect(): projection = jnp.sum(current * pulled, axis=1, keepdims=True)]
    psum x1 -> x0, blocking collectives: 9.26 us -> none  [on_device(): energy_now = lax.psum(local_energy, 'gz') / total_sites]
    unnamed x18, local copies, waits for them, and re-layouts: 1.19 us -> 9.28 us
    mul x2 -> x0, other arithmetic: 4.76 us -> none  [the longest x1 3.4 us: heat_bath(): side * jnp.cos(angle_draw)]
  transfers between devices with their start and end apart: 18 -> 0, of which waited for: 11 -> 0; matrix products, arithmetic and copies ran while one was open for 11% -> 0% of each run, Pallas kernels for 0% -> 0%
where the time goes in v1:
time: 79.9 us; the launch traced here: 79.5 us
  Pallas kernels  69.6 us (87%)
  local copies, waits for them, and re-layouts  9.28 us (12%)
    pallas_call x1, Pallas kernels, on_device(): pl.pallas_call(functools.partial(kernel, (count, planes, rows, width, n,...  69.6 us
    unnamed x18, local copies, waits for them, and re-layouts  9.28 us

profile of v1, /device:TPU:1, one launch (start us, length us, event | category | flops | bytes accessed | tf_op | source)
XLA Modules:
  0.0 79.5 jit_solution(6016567232557797279)
XLA Ops:
  0.6 0.0 copy-start
  0.6 1.4 %copy-done = f32[2,3,4,128,128]{4,3,2,1,0:T(8,128)S(1)} copy-done((f32[2,3,4,128,128]{4,3,2,1,0:T(8,128)S(1)}, f32[2,3,4,128,128]{4,3,2,1,0:T(8,128)}, u32[]{:S(2)}) %copy-start) | copy-done | bytes 1572888
  2.0 0.0 copy-start.1
  2.0 1.1 %copy-done.1 = f32[3,4,128,128]{3,2,1,0:T(8,128)S(1)} copy-done((f32[3,4,128,128]{3,2,1,0:T(8,128)S(1)}, f32[3,4,128,128]{3,2,1,0:T(8,128)}, u32[]{:S(2)}) %copy-start.1) | copy-done | bytes 786456
  3.2 0.0 copy-start.2
  3.2 1.0 %copy-done.2 = f32[2,4,128,128]{3,2,1,0:T(8,128)S(1)} copy-done((f32[2,4,128,128]{3,2,1,0:T(8,128)S(1)}, f32[2,4,128,128]{3,2,1,0:T(8,128)}, u32[]{:S(2)}) %copy-start.2) | copy-done | bytes 524312
  4.2 0.0 copy-start.3
  4.2 1.0 %copy-done.3 = f32[2,4,128,128]{3,2,1,0:T(8,128)S(1)} copy-done((f32[2,4,128,128]{3,2,1,0:T(8,128)S(1)}, f32[2,4,128,128]{3,2,1,0:T(8,128)}, u32[]{:S(2)}) %copy-start.3) | copy-done | bytes 524312
  5.3 0.0 copy-start.4
  5.3 1.0 %copy-done.4 = f32[2,4,128,128]{3,2,1,0:T(8,128)S(1)} copy-done((f32[2,4,128,128]{3,2,1,0:T(8,128)S(1)}, f32[2,4,128,128]{3,2,1,0:T(8,128)}, u32[]{:S(2)}) %copy-start.4) | copy-done | bytes 524312
  6.3 0.0 copy-start.5
  6.3 0.7 copy-done.5
  7.0 0.0 copy-start.6
  7.0 0.7 copy-done.6
  7.6 0.0 copy-start.7
  7.6 0.7 copy-done.7
  8.3 69.6 %shard_map.95 = (f32[2,3,4,128,128]{4,3,2,1,0:T(8,128)S(1)}, f32[2]{0:T(128)S(1)}) custom-call(f32[2,3,4,128,128]{4,3,2,1,0:T(8,128)S(1)} %copy-done, f32[3,4,128,128]{3,2,1,0:T(8,128)S(1)} %copy-done.1, f32[2]{0:T(128)S(1)} %copy-done.5, s32[2]{0:T(128)S(1)} %copy-done.6, f32[2,4,128,128]{3,2,1,0:T(8,128)S(1)} %copy-done.2, ...), custom_call_target="tpu_custom_call" | custom-call | tf_op jit(solution)/shard_map/pallas_call | solution.py:489
  77.9 1.1 %copy.12 = f32[2,3,4,128,128]{4,3,2,1,0:T(8,128)} copy(f32[2,3,4,128,128]{4,3,2,1,0:T(8,128)S(1)} %get-tuple-element.4) | data formatting | bytes 3145728
  79.0 0.5 copy.13
Async XLA Ops:
  0.6 1.4 %copy-start = (f32[2,3,4,128,128]{4,3,2,1,0:T(8,128)S(1)}, f32[2,3,4,128,128]{4,3,2,1,0:T(8,128)}, u32[]{:S(2)}) copy-start(f32[2,3,4,128,128]{4,3,2,1,0:T(8,128)} %spin_hbm.1) | copy-start | bytes 4718596
  2.0 1.1 %copy-start.1 = (f32[3,4,128,128]{3,2,1,0:T(8,128)S(1)}, f32[3,4,128,128]{3,2,1,0:T(8,128)}, u32[]{:S(2)}) copy-start(f32[3,4,128,128]{3,2,1,0:T(8,128)} %coup_hbm.1) | copy-start | bytes 2359300
  3.2 1.0 %copy-start.2 = (f32[2,4,128,128]{3,2,1,0:T(8,128)S(1)}, f32[2,4,128,128]{3,2,1,0:T(8,128)}, u32[]{:S(2)}) copy-start(f32[2,4,128,128]{3,2,1,0:T(8,128)} %level_hbm.1) | copy-start | bytes 1572868
  4.2 1.0 %copy-start.3 = (f32[2,4,128,128]{3,2,1,0:T(8,128)S(1)}, f32[2,4,128,128]{3,2,1,0:T(8,128)}, u32[]{:S(2)}) copy-start(f32[2,4,128,128]{3,2,1,0:T(8,128)} %height_hbm.1) | copy-start | bytes 1572868
  5.3 1.0 %copy-start.4 = (f32[2,4,128,128]{3,2,1,0:T(8,128)S(1)}, f32[2,4,128,128]{3,2,1,0:T(8,128)}, u32[]{:S(2)}) copy-start(f32[2,4,128,128]{3,2,1,0:T(8,128)} %angle_hbm.1) | copy-start | bytes 1572868
  6.3 0.7 copy-start.5
  7.0 0.7 copy-start.6
  7.6 0.7 copy-start.7

commit v2 on v1

--- a/solution.py
+++ b/solution.py
@@ -110,8 +110,16 @@
         pltpu.make_async_copy(src, dst, in_sem.at[i])
         for i, (src, dst) in enumerate(
             (
-                (spin_hbm, spin_in),
+                (spin_hbm.at[:, :, pl.ds(0, 1)], spin_in.at[:, :, pl.ds(0, 1)]),
+                (
+                    spin_hbm.at[:, :, pl.ds(planes - 1, 1)],
+                    spin_in.at[:, :, pl.ds(planes - 1, 1)],
+                ),
                 (coup_hbm, coup_in),
+                (
+                    spin_hbm.at[:, :, pl.ds(1, planes - 2)],
+                    spin_in.at[:, :, pl.ds(1, planes - 2)],
+                ),
                 (level_hbm, level_in),
                 (height_hbm, height_in),
                 (angle_hbm, angle_in),
@@ -189,11 +197,12 @@
             lax.fori_loop(0, count * (planes - 2), step, 0)
 
     loads[0].wait()
+    loads[1].wait()
     for r in range(count):
         edges(r, pack_spin)
         for side in (0, 1):
             halo(0, r, side).start()
-    loads[1].wait()
+    loads[2].wait()
     bond = pltpu.make_async_remote_copy(
         src_ref=coup_in.at[2, planes - 1],
         dst_ref=below_bond,
@@ -203,6 +212,7 @@
         device_id_type=MESH,
     )
     bond.start()
+    loads[3].wait()
     inner(pack_spin)
 
     def pack_bonds(i, carry):
@@ -318,7 +328,7 @@
                 halo(x + 1, r, side).start()
         inner(work)
         if x == 0:
-            for load in loads[2:]:
+            for load in loads[4:]:
                 load.wait()
         for r in range(count):
             if r % (2 * OR_SWEEPS) == x:
@@ -515,7 +525,7 @@
             pltpu.VMEM((3, 8, width), f32),
             pltpu.VMEM((3, 8, width), f32),
             pltpu.VMEM((2, 3, planes, rows, width), f32),
-            dma((5,)),
+            dma((7,)),
             dma((2,)),
             dma((HALVES, count, 2)),
             dma((HALVES, count, 2)),
@@ -527,7 +537,7 @@
             dma((planes, 2)),
         ],
         compiler_params=pltpu.CompilerParams(
-            collective_id=0, has_side_effects=True, vmem_limit_bytes=48 * 1024 * 1024
+            collective_id=0, has_side_effects=True, vmem_limit_bytes=60 * 1024 * 1024
         ),
     )(spin, coup, beta, order, level, height, angle, bits)
 

time: 79.9 us -> 74 us (0.926)
  local copies, waits for them, and re-layouts: 9.28 us -> 3.22 us
    unnamed x18 -> x4, local copies, waits for them, and re-layouts: 9.28 us -> 3.22 us
where the time goes in v2:
time: 74 us; the launch traced here: 73.8 us
  Pallas kernels  70 us (95%)
  local copies, waits for them, and re-layouts  3.22 us (4%)
    pallas_call x1, Pallas kernels, on_device(): pl.pallas_call(functools.partial(kernel, (count, planes, rows, width, n,...  70 us
    unnamed x4, local copies, waits for them, and re-layouts  3.22 us

profile of v2, /device:TPU:1, one launch (start us, length us, event | category | flops | bytes accessed | tf_op | source)
XLA Modules:
  0.0 73.8 jit_solution(9692090344065093232)
XLA Ops:
  0.6 70.0 %shard_map.95 = (f32[2,3,4,128,128]{4,3,2,1,0:T(8,128)}, f32[2]{0:T(128)}) custom-call(f32[2,3,4,128,128]{4,3,2,1,0:T(8,128)} %spin_hbm.1, f32[3,4,128,128]{3,2,1,0:T(8,128)} %coup_hbm.1, f32[2]{0:T(128)} %beta_ref.1, s32[2]{0:T(128)} %order_ref.1, f32[2,4,128,128]{3,2,1,0:T(8,128)} %level_hbm.1, f32[2,4,128,128]{3,2,1,0:T(8,128)} %height_hbm.1, ...), custom_call_target="tpu_custom_call" | custom-call | tf_op jit(solution)/shard_map/pallas_call | solution.py:499
  70.6 0.0 copy-start
  70.6 2.7 %copy.12 = f32[2,3,4,128,128]{4,3,2,1,0:T(8,128)} copy(f32[2,3,4,128,128]{4,3,2,1,0:T(8,128)} %get-tuple-element.4) | data formatting | bytes 3145728
  73.3 0.0 copy-done
  73.3 0.5 copy.13
Async XLA Ops:
  70.6 2.7 %copy-start = (f32[2]{0:T(128)S(1)}, f32[2]{0:T(128)}, u32[]{:S(2)}) copy-start(f32[2]{0:T(128)} %get-tuple-element.5) | copy-start | bytes 28

commit v3 on v2

--- a/solution.py
+++ b/solution.py
@@ -72,7 +72,7 @@
     level_in,
     height_in,
     angle_in,
-    below_bond,
+    lifted,
     sp,
     xo,
     xr,
@@ -88,7 +88,6 @@
     trecv,
     rbuf,
     in_sem,
-    bond_sem,
     hsend,
     hrecv,
     esend,
@@ -115,7 +114,12 @@
                     spin_hbm.at[:, :, pl.ds(planes - 1, 1)],
                     spin_in.at[:, :, pl.ds(planes - 1, 1)],
                 ),
-                (coup_hbm, coup_in),
+                (coup_hbm.at[2, planes - 1], coup_in.at[2, planes - 1]),
+                (coup_hbm.at[pl.ds(0, 2)], coup_in.at[pl.ds(0, 2)]),
+                (
+                    coup_hbm.at[2, pl.ds(0, planes - 1)],
+                    coup_in.at[2, pl.ds(0, planes - 1)],
+                ),
                 (
                     spin_hbm.at[:, :, pl.ds(1, planes - 2)],
                     spin_in.at[:, :, pl.ds(1, planes - 2)],
@@ -171,22 +175,19 @@
 
     def halo(x, r, side):
         c = 1 - x % 2
-        source, target = (1, planes + 1) if side == 0 else (planes, 0)
+        plain = sp.at[c, r, :, 1, pl.ds(PAD, k), :]
         return pltpu.make_async_remote_copy(
-            src_ref=sp.at[c, r, :, source, pl.ds(PAD, k), :],
-            dst_ref=sp.at[c, r, :, target, pl.ds(PAD, k), :],
+            src_ref=plain if side == 0 else lifted.at[c, r],
+            dst_ref=sp.at[c, r, :, planes + 1 if side == 0 else 0, pl.ds(PAD, k), :],
             send_sem=hsend.at[x, r, side],
             recv_sem=hrecv.at[x, r, side],
             device_id={"gz": down if side == 0 else up},
             device_id_type=MESH,
         )
 
-    def edges(r, action):
-        def step(i, carry):
-            action(r, i * (planes - 1))
-            return carry
-
-        lax.fori_loop(0, 2, step, 0)
+    def lift(c, r, d, start, value):
+        part = pl.ds(start, value.shape[0])
+        lifted[c, r, d, part, :] = zu[c, r, planes - 1, part, :] * value
 
     def inner(action):
         def step(i, carry):
@@ -196,23 +197,21 @@
         if planes > 2:
             lax.fori_loop(0, count * (planes - 2), step, 0)
 
-    loads[0].wait()
-    loads[1].wait()
+    for load in loads[:3]:
+        load.wait()
     for r in range(count):
-        edges(r, pack_spin)
-        for side in (0, 1):
-            halo(0, r, side).start()
-    loads[2].wait()
-    bond = pltpu.make_async_remote_copy(
-        src_ref=coup_in.at[2, planes - 1],
-        dst_ref=below_bond,
-        send_sem=bond_sem.at[0],
-        recv_sem=bond_sem.at[1],
-        device_id={"gz": up},
-        device_id_type=MESH,
-    )
-    bond.start()
-    loads[3].wait()
+        pack_spin(r, 0)
+        halo(0, r, 0).start()
+        e = parity(r, planes - 1, k)
+        even, odd = halves(coup_in, (2, planes - 1), 0, k)
+        zu[0, r, planes - 1] = jnp.where(e, odd, even)
+        zu[1, r, planes - 1] = jnp.where(e, even, odd)
+        pack_spin(r, planes - 1)
+        for d in range(3):
+            lift(1, r, d, 0, sp[1, r, d, planes, pl.ds(PAD, k), :])
+        halo(0, r, 1).start()
+    for load in loads[3:6]:
+        load.wait()
     inner(pack_spin)
 
     def pack_bonds(i, carry):
@@ -229,9 +228,6 @@
         yi[r, z] = even
         yo[0, r, z] = jnp.where(e, odd, before)
         yo[1, r, z] = jnp.where(e, before, odd)
-        even, odd = halves(coup_in, (2, z), 0, k)
-        zu[0, r, z] = jnp.where(e, odd, even)
-        zu[1, r, z] = jnp.where(e, even, odd)
         return carry
 
     def pack_lower(i, carry):
@@ -240,16 +236,15 @@
         even, odd = halves(coup_in, (2, z - 1), 0, k)
         zd[0, r, z] = jnp.where(e, odd, even)
         zd[1, r, z] = jnp.where(e, even, odd)
+        zu[0, r, z - 1] = jnp.where(e, even, odd)
+        zu[1, r, z - 1] = jnp.where(e, odd, even)
         return carry
 
     lax.fori_loop(0, count * planes, pack_bonds, 0)
     lax.fori_loop(0, count * (planes - 1), pack_lower, 0)
-    bond.wait()
     for r in range(count):
-        e = parity(r, 0, k)
-        even, odd = halves(below_bond, (), 0, k)
-        zd[0, r, 0] = jnp.where(e, odd, even)
-        zd[1, r, 0] = jnp.where(e, even, odd)
+        for c in (0, 1):
+            zd[c, r, 0] = jnp.ones((k, width), jnp.float32)
 
     def pull(c, r, z, start):
         o = 1 - c
@@ -270,14 +265,16 @@
             pulled.append(total)
         return pulled
 
-    def relax(c, r, z):
+    def relax(c, r, z, lifting=False):
         for start in range(0, k, chunk):
             pulled = pull(c, r, z, start)
             current = [sp[c, r, d, z + 1, pl.ds(PAD + start, chunk), :] for d in range(3)]
             for d, value in enumerate(reflect(current, pulled)):
                 put_spin(c, r, d, z, start, value)
-
-    def heat(c, r, z):
+                if lifting:
+                    lift(c, r, d, start, value)
+
+    def heat(c, r, z, lifting=False):
         for start in range(0, k, chunk):
             part = pl.ds(start, chunk)
             pulled = pull(c, r, z, start)
@@ -285,6 +282,8 @@
             renewed = heat_bath(pulled, beta_ref[r], lv[c, r, z, part, :], trial)
             for d, value in enumerate(renewed):
                 put_spin(c, r, d, z, start, value)
+                if lifting:
+                    lift(c, r, d, start, value)
             if c == 1:
                 terms = dot3(renewed, pulled)
                 eacc[r] = eacc[r] + sum(terms[j : j + 8] for j in range(0, chunk, 8))
@@ -311,24 +310,23 @@
 
         lax.fori_loop(0, planes, step, 0)
 
-    def take_halo(x, r):
-        for side in (0, 1):
-            halo(x, r, side).wait_recv()
-            if x >= 1:
-                halo(x - 1, r, side).wait_send()
+    def take_halo(x, r, side):
+        halo(x, r, 1 - side).wait_recv()
+        if x >= 1:
+            halo(x - 1, r, side).wait_send()
 
     eacc[...] = jnp.zeros_like(eacc)
     for x in range(HALVES - 1):
         c = x % 2
         work = functools.partial(relax if x < 2 * OR_SWEEPS else heat, c)
         for r in range(count):
-            take_halo(x, r)
-            edges(r, work)
-            for side in (0, 1):
+            for side, z in ((0, 0), (1, planes - 1)):
+                take_halo(x, r, side)
+                work(r, z, lifting=side == 1)
                 halo(x + 1, r, side).start()
         inner(work)
         if x == 0:
-            for load in loads[4:]:
+            for load in loads[6:]:
                 load.wait()
         for r in range(count):
             if r % (2 * OR_SWEEPS) == x:
@@ -384,8 +382,9 @@
     outside = [0, planes - 1]
     finish(middle)
     for r in range(count):
-        take_halo(x, r)
-        edges(r, work)
+        for side, z in ((0, 0), (1, planes - 1)):
+            take_halo(x, r, side)
+            work(r, z)
     swaps = []
     for d in range(1, n):
         swaps.append(
@@ -510,7 +509,7 @@
             pltpu.VMEM(level.shape, f32),
             pltpu.VMEM(level.shape, f32),
             pltpu.VMEM(level.shape, f32),
-            pltpu.VMEM((rows, width), f32),
+            pltpu.VMEM((2, count, 3, k, width), f32),
             pltpu.VMEM((2, count, 3, planes + 2, k + 2 * PAD, width), f32),
             bonds,
             bonds,
@@ -525,8 +524,7 @@
             pltpu.VMEM((3, 8, width), f32),
             pltpu.VMEM((3, 8, width), f32),
             pltpu.VMEM((2, 3, planes, rows, width), f32),
-            dma((7,)),
-            dma((2,)),
+            dma((9,)),
             dma((HALVES, count, 2)),
             dma((HALVES, count, 2)),
             dma((n - 1,)),

time: 74 us -> 71.6 us (0.968)
  Pallas kernels: 70 us -> 67.6 us
    pallas_call x1, Pallas kernels: 70 us -> 67.6 us  [on_device(): pl.pallas_call(functools.partial(kernel, (count, planes, rows, width, n,...]
where the time goes in v3:
time: 71.6 us; the launch traced here: 71.5 us
  Pallas kernels  67.6 us (94%)
  local copies, waits for them, and re-layouts  3.22 us (4%)
    pallas_call x1, Pallas kernels, on_device(): pl.pallas_call(functools.partial(kernel, (count, planes, rows, width, n,...  67.6 us
    unnamed x4, local copies, waits for them, and re-layouts  3.22 us

profile of v3, /device:TPU:1, one launch (start us, length us, event | category | flops | bytes accessed | tf_op | source)
XLA Modules:
  0.0 71.5 jit_solution(3578226624176878060)
XLA Ops:
  0.6 67.6 %shard_map.95 = (f32[2,3,4,128,128]{4,3,2,1,0:T(8,128)}, f32[2]{0:T(128)}) custom-call(f32[2,3,4,128,128]{4,3,2,1,0:T(8,128)} %spin_hbm.1, f32[3,4,128,128]{3,2,1,0:T(8,128)} %coup_hbm.1, f32[2]{0:T(128)} %beta_ref.1, s32[2]{0:T(128)} %order_ref.1, f32[2,4,128,128]{3,2,1,0:T(8,128)} %level_hbm.1, f32[2,4,128,128]{3,2,1,0:T(8,128)} %height_hbm.1, ...), custom_call_target="tpu_custom_call" | custom-call | tf_op jit(solution)/shard_map/pallas_call | solution.py:498
  68.3 0.0 copy-start
  68.3 2.7 %copy.12 = f32[2,3,4,128,128]{4,3,2,1,0:T(8,128)} copy(f32[2,3,4,128,128]{4,3,2,1,0:T(8,128)} %get-tuple-element.4) | data formatting | bytes 3145728
  71.0 0.0 copy-done
  71.0 0.5 copy.13
Async XLA Ops:
  68.3 2.7 %copy-start = (f32[2]{0:T(128)S(1)}, f32[2]{0:T(128)}, u32[]{:S(2)}) copy-start(f32[2]{0:T(128)} %get-tuple-element.5) | copy-start | bytes 28

commit v4 on v3

--- a/solution.py
+++ b/solution.py
@@ -381,10 +381,12 @@
     middle = list(range(1, planes - 1))
     outside = [0, planes - 1]
     finish(middle)
-    for r in range(count):
-        for side, z in ((0, 0), (1, planes - 1)):
+    for side, z in ((0, 0), (1, planes - 1)):
+        for r in range(count):
             take_halo(x, r, side)
             work(r, z)
+        if side == 0:
+            finish([z])
     swaps = []
     for d in range(1, n):
         swaps.append(
@@ -399,7 +401,7 @@
         )
     for swap in swaps:
         swap.start()
-    finish(outside)
+    finish([planes - 1])
 
     for swap in swaps:
         swap.wait()

time: 71.6 us -> 71.4 us (level)
  no operation moved by 1% of the time
where the time goes in v4:
time: 71.4 us; the launch traced here: 71.2 us
  Pallas kernels  67.4 us (94%)
  local copies, waits for them, and re-layouts  3.22 us (5%)
    pallas_call x1, Pallas kernels, on_device(): pl.pallas_call(functools.partial(kernel, (count, planes, rows, width, n,...  67.4 us
    unnamed x4, local copies, waits for them, and re-layouts  3.22 us

profile of v4, /device:TPU:1, one launch (start us, length us, event | category | flops | bytes accessed | tf_op | source)
XLA Modules:
  0.0 71.2 jit_solution(18080509525212447783)
XLA Ops:
  0.6 67.4 %shard_map.95 = (f32[2,3,4,128,128]{4,3,2,1,0:T(8,128)}, f32[2]{0:T(128)}) custom-call(f32[2,3,4,128,128]{4,3,2,1,0:T(8,128)} %spin_hbm.1, f32[3,4,128,128]{3,2,1,0:T(8,128)} %coup_hbm.1, f32[2]{0:T(128)} %beta_ref.1, s32[2]{0:T(128)} %order_ref.1, f32[2,4,128,128]{3,2,1,0:T(8,128)} %level_hbm.1, f32[2,4,128,128]{3,2,1,0:T(8,128)} %height_hbm.1, ...), custom_call_target="tpu_custom_call" | custom-call | tf_op jit(solution)/shard_map/pallas_call | solution.py:500
  68.0 0.0 copy-start
  68.0 2.7 %copy.12 = f32[2,3,4,128,128]{4,3,2,1,0:T(8,128)} copy(f32[2,3,4,128,128]{4,3,2,1,0:T(8,128)} %get-tuple-element.4) | data formatting | bytes 3145728
  70.7 0.0 copy-done
  70.7 0.5 copy.13
Async XLA Ops:
  68.0 2.7 %copy-start = (f32[2]{0:T(128)S(1)}, f32[2]{0:T(128)}, u32[]{:S(2)}) copy-start(f32[2]{0:T(128)} %get-tuple-element.5) | copy-start | bytes 28
